TPU v7x, 32 devices: a whole 2x2x4 slice. The times are simulated.
32 devices in a mesh: groups: 2 (over x), frame: 8 (over z, y), band: 2 (over core).
Axes of the slice: x: 2, y: 2, z: 4, core: 2. Of those that a mesh axis runs over, the one named last changes fastest.
Arguments:
- hidden_in: bfloat16 [16, 1536, 1152], P(('groups', 'frame'), 'band'), parts along dimension 0, may hold values from -6 to 6
- latents: float32 [16, 192, 128], P(('groups', 'frame'), 'band'), parts along dimension 0, may hold values from -6 to 6
- fresh_noise: float32 [384, 128], P(('groups', 'band')), parts along dimension 0, may hold values from -6 to 6
- level_index: int32 [16], P(('groups', 'frame')), parts along dimension 0, may hold values from 1 to 31
- time_table: int32 [32], replicated, may hold values from 0 to 999, as said below
- frame_offset: int32 [2], P('groups'), parts along dimension 0, may hold values from 0 to 1023
- mod_table: float32 [3456], replicated, may hold values from -3 to 3
- time_weight: bfloat16 [128, 3456], replicated, may hold values from -0.5 to 0.5
- spatial_qkv: bfloat16 [1152, 1728], replicated, may hold values from -6 to 6
- spatial_out: bfloat16 [576, 1152], replicated, may hold values from -0.25 to 0.25
- temporal_qkv: bfloat16 [1152, 1728], replicated, may hold values from -6 to 6
- temporal_out: bfloat16 [576, 1152], replicated, may hold values from -0.25 to 0.25
- final_gain: float32 [1152], replicated, may hold values from 0.5 to 1.5
- out_weight: bfloat16 [1152, 16], replicated, may hold values from -0.1875 to 0.1875
Outputs:
- hidden_out: bfloat16 [16, 1536, 1152], P(('groups', 'frame'), 'band'), parts along dimension 0
- velocity: float32 [16, 192, 128], P(('groups', 'frame'), 'band'), parts along dimension 0
- next_latents: float32 [16, 192, 128], P(('groups', 'frame'), 'band'), parts along dimension 0
There are 2 independent parts, one for each index of `groups`. A program takes and returns all parts, laid end to end along the dimension named above; an argument that names none is the same for every part. Nothing has to cross between parts.
Inputs may be any that keep to these rules, and one draw needn't show every extreme that they name: `time_table`: entries rise strictly along the table, from 0 at the first entry to 999 at the last.
All inputs are finite; a program needn't handle non-finite values.
Results may differ from a plain program's by a relative error of at most 0.025.
Values may be sent and summed in bfloat16 or wider, within the bound.
No kernel may reach another device: no remote copies, remote signals or barrier semaphores. Data moves between devices by JAX's collectives and lax.ppermute only.
A program may use at most 128 MiB of HBM per device.

v0:
```python
import math
import jax
import jax.numpy as jnp
from jax import lax
from jax.sharding import PartitionSpec as P

HEAD_SIZE = 72
epsilon = 1e-06


def from_behind(value, axis, steps):
    count = lax.axis_size(axis)
    initial, last = (max(0, -steps), min(count, count - steps))
    return lax.ppermute(value, axis, [(source, source + steps) for source in range(initial, last)])


def layer_norm(values):
    average = jnp.mean(values, axis=-1, keepdims=True)
    centred = values - average
    variance = jnp.mean(centred * centred, axis=-1, keepdims=True)
    return centred * lax.rsqrt(variance + epsilon)


def sinusoid(position, feature_count, first_sine):
    half_width = feature_count // 2
    frequency = jnp.exp(-math.log(10000.0) * jnp.arange(half_width, dtype=jnp.float32) / half_width)
    angles = position.astype(jnp.float32)[:, None] * frequency[None, :]
    if first_sine:
        return jnp.concatenate([jnp.sin(angles), jnp.cos(angles)], axis=-1)
    return jnp.concatenate([jnp.cos(angles), jnp.sin(angles)], axis=-1)


def mix_frames(rows, head_count):
    frame_count = rows.shape[0]
    item_count = rows.shape[1]
    parted = rows.reshape(frame_count, item_count, 3, head_count, HEAD_SIZE)
    attention_scores = jnp.einsum(
        "fnhd,gnhd->nhfg", parted[:, :, 0], parted[:, :, 1], preferred_element_type=jnp.float32
    ) / math.sqrt(HEAD_SIZE)
    row_max = jnp.max(attention_scores, axis=-1, keepdims=True)
    attention_weight = jnp.exp(attention_scores - row_max).astype(jnp.bfloat16)
    denominator = jnp.sum(attention_weight, axis=-1, dtype=jnp.float32)
    weighted_sum = jnp.einsum(
        "nhfg,gnhd->fnhd", attention_weight, parted[:, :, 2], preferred_element_type=jnp.float32
    )
    mixed = weighted_sum / jnp.transpose(denominator, (2, 0, 1))[..., None]
    return mixed.astype(jnp.bfloat16).reshape(frame_count, item_count, head_count * HEAD_SIZE)


def body(
    hidden_in,
    latents,
    fresh_noise,
    level_index,
    time_table,
    frame_offset,
    mod_table,
    time_weight,
    spatial_qkv,
    spatial_out,
    temporal_qkv,
    temporal_out,
    final_gain,
    out_weight,
):
    tokens = hidden_in.shape[1]
    model_width = hidden_in.shape[2]
    attended = spatial_out.shape[0]
    head_count = attended // HEAD_SIZE
    peers = lax.axis_size("frame")
    table_index = jnp.arange(time_table.shape[0], dtype=jnp.int32)
    now_steps = jnp.sum(
        jnp.where(table_index[None, :] == level_index[:, None], time_table[None, :], 0), axis=1
    )
    next_steps = jnp.sum(
        jnp.where(table_index[None, :] == level_index[:, None] - 1, time_table[None, :], 0), axis=1
    )
    activated = jax.nn.silu(sinusoid(now_steps, time_weight.shape[0], False)).astype(jnp.bfloat16)
    modulation = mod_table[None, :] + jnp.dot(
        activated, time_weight, preferred_element_type=jnp.float32
    )
    shift_part = modulation[:, :model_width]
    scale_part = modulation[:, model_width : 2 * model_width]
    gate_part = modulation[:, 2 * model_width :]
    inputs = hidden_in[0].astype(jnp.float32)
    normed = (layer_norm(inputs) * (1.0 + scale_part) + shift_part).astype(jnp.bfloat16)
    projected = jnp.dot(normed, spatial_qkv, preferred_element_type=jnp.float32).astype(
        jnp.bfloat16
    )
    query_rows = projected[:, :attended].reshape(tokens, head_count, HEAD_SIZE)
    key_value = projected[:, attended:]
    block_rows = lax.all_gather(key_value, "band", axis=0, tiled=True)
    row_max = jnp.full((head_count, tokens), -1e30, jnp.float32)
    row_count = block_rows.shape[0]
    key_matrix_rows = block_rows[:, :attended].reshape(row_count, head_count, HEAD_SIZE)
    value_matrix_rows = block_rows[:, attended:].reshape(row_count, head_count, HEAD_SIZE)
    attention_scores = jnp.einsum(
        "ubg,wbg->buw", query_rows, key_matrix_rows, preferred_element_type=jnp.float32
    ) / math.sqrt(HEAD_SIZE)
    new_max = jnp.maximum(row_max, jnp.max(attention_scores, axis=-1))
    attention_weight = jnp.exp(attention_scores - new_max[:, :, None]).astype(jnp.bfloat16)
    denominator = jnp.sum(attention_weight, axis=-1, dtype=jnp.float32)
    weighted_sum = jnp.einsum(
        "leq,qlr->ler", attention_weight, value_matrix_rows, preferred_element_type=jnp.float32
    )
    row_max, denominator, weighted_sum = (new_max, denominator, weighted_sum)
    spatial_mixed = (
        jnp.transpose(weighted_sum / denominator[:, :, None], (1, 0, 2))
        .reshape(tokens, attended)
        .astype(jnp.bfloat16)
    )
    residual = inputs + gate_part * jnp.dot(
        spatial_mixed, spatial_out, preferred_element_type=jnp.float32
    )
    position = lax.axis_index("frame") + frame_offset
    placed = sinusoid(position, model_width, True)
    temporal_in = (residual + placed).astype(jnp.bfloat16)
    spread_rows = temporal_in.reshape(1, peers, tokens // peers, model_width)
    gathered = lax.all_to_all(spread_rows, "frame", split_axis=1, concat_axis=0, tiled=True)
    frame_count = gathered.shape[0]
    item_count = gathered.shape[2]
    rows = jnp.dot(
        gathered.reshape(frame_count * item_count, model_width),
        temporal_qkv,
        preferred_element_type=jnp.float32,
    ).astype(jnp.bfloat16)
    mixed = mix_frames(rows.reshape(frame_count, item_count, 3 * attended), head_count)
    mixed_rows = mixed.reshape(frame_count, 1, item_count, attended)
    mixed_pairs = mixed_rows.reshape(mixed_rows.shape[0], 1, mixed_rows.shape[2] // 2, 2 * attended)
    returned = lax.all_to_all(mixed_pairs, "frame", split_axis=0, concat_axis=1, tiled=True)
    temporal_mixed = returned.reshape(tokens, attended)
    residual = residual + gate_part * jnp.dot(
        temporal_mixed, temporal_out, preferred_element_type=jnp.float32
    )
    hidden_out = residual.astype(jnp.bfloat16)[None]
    final_rows = (layer_norm(residual) * final_gain).astype(jnp.bfloat16)
    velocity = jnp.dot(final_rows, out_weight, preferred_element_type=jnp.float32).reshape(
        1, latents.shape[1], 128
    )
    time_delta = (next_steps - now_steps).astype(jnp.float32) / 1000.0
    update = latents + time_delta[:, None, None] * velocity
    shifted = from_behind(update.astype(jnp.bfloat16), "frame", 1).astype(update.dtype)
    next_latents = jnp.where(lax.axis_index("frame") == 0, fresh_noise[None], shifted)
    return (hidden_out, velocity, next_latents)


def solution(mesh):
    placed = (
        P(("groups", "frame"), "band", None),
        P(("groups", "frame"), "band", None),
        P(("groups", "band"), None),
        P(("groups", "frame")),
        P(),
        P("groups"),
        P(),
        P(),
        P(),
        P(),
        P(),
        P(),
        P(),
        P(),
    )
    return jax.shard_map(
        body,
        mesh=mesh,
        in_specs=placed,
        out_specs=(
            P(("groups", "frame"), "band", None),
            P(("groups", "frame"), "band", None),
            P(("groups", "frame"), "band", None),
        ),
        check_vma=False,
    )
```

profile of v0, /device:TPU:0, one launch (start us, length us, event | category | flops | bytes accessed | tf_op | source)
XLA Modules:
  0.0 232.9 jit_solution(8526192935074219680)
XLA Ops:
  8.0 1.4 fusion.32
  10.2 1.5 convolution_reduce_fusion
  11.7 0.7 add.73
  12.5 1.8 convert_reduce_fusion.1
  14.9 5.9 %convolution_convert_fusion.1 = bf16[768,1728]{0,1:T(8,128)(2,1)S(1)} fusion(bf16[1152,1728]{0,1:T(8,128)(2,1)} %param.22, bf16[1,768,1152]{2,1,0:T(8,128)(2,1)S(1)} %copy-done.1, f32[1152]{0:T(1024)S(1)} %get-tuple-element.4, f32[1152]{0:T(1024)S(1)} %get-tuple-element.5, f32[768]{0:T(1024)S(1)} %add_rsqrt_fusion.1, f32[768]{0:T(1024)S(1)} %broadcast_multiply_fusion.1), kind=kOutput, calls=%fused_computation.21 | convolution fusion | flops 3064283136 | bytes 8420352 | tf_op jit(solution)/shard_map/dot_general | solution.py:87
  20.8 1.5 copy-done.2
  22.3 1.3 slice.44
  24.5 14.7 %all-gather.2.cloned.1.call-done = bf16[1536,1152]{0,1:T(8,128)(2,1)} async-done(((bf16[768,1152]{0,1:T(8,128)(2,1)}), bf16[1536,1152]{0,1:T(8,128)(2,1)}) %all-gather.2.cloned.1.call-update) | async-done | bytes 3538960 | tf_op jit(solution)/shard_map/all_gather | solution.py:92
  39.3 3.5 %fusion.45 = (bf16[1536,576]{0,1:T(8,128)(2,1)S(1)}, bf16[1536,576]{0,1:T(8,128)(2,1)}) fusion(bf16[1536,1152]{0,1:T(8,128)(2,1)} %all-gather.2.cloned.1.call-done), kind=kLoop, calls=%fused_computation.79 | loop fusion | bytes 7077888 | tf_op jit(solution)/shard_map/slice | solution.py:95
  42.8 14.8 %multiply_reduce_fusion = (f32[8,768]{1,0:T(8,128)S(1)}, f32[8,768,1536]{2,1,0:T(8,128)}) fusion(bf16[768,8,72]{0,2,1:T(8,128)(2,1)S(1)} %bitcast.79, bf16[1536,8,72]{0,2,1:T(8,128)(2,1)S(1)} %bitcast.78), kind=kOutput, calls=%fused_computation.3 | convolution fusion | flops 1377822720 | bytes 40427520 | tf_op jit(solution)/shard_map/ubg,wbg->buw/dot_general | solution.py:97
  57.6 16.7 %convert_reduce_fusion = f32[8,768]{1,0:T(8,128)S(1)} fusion(f32[8,768]{1,0:T(8,128)S(1)} %broadcast_maximum_fusion, f32[8,768,1536]{2,1,0:T(8,128)} %get-tuple-element.16), kind=kLoop, calls=%fused_computation.1 | loop fusion | flops 47179776 | bytes 37797888 | tf_op jit(solution)/shard_map/reduce_sum | solution.py:102
  74.3 16.7 %fusion.13 = bf16[768,8,72]{0,2,1:T(8,128)(2,1)} fusion(bf16[1536,8,72]{0,2,1:T(8,128)(2,1)} %bitcast.81, f32[8,768,1536]{2,1,0:T(8,128)} %get-tuple-element.16, f32[8,768]{1,0:T(8,128)S(1)} %broadcast_maximum_fusion, f32[768,8]{0,1:T(8,128)S(1)} %bitcast.85), kind=kOutput, calls=%fused_computation.26 | convolution fusion | flops 1388150784 | bytes 40452096 | tf_op jit(solution)/shard_map/leq,qlr->ler/dot_general | solution.py:103
  91.0 5.0 %add_convert_fusion = (bf16[768,1152]{1,0:T(8,128)(2,1)S(1)}, f32[768,1152]{1,0:T(8,128)}) fusion(f32[1152]{0:T(1024)S(1)} %maximum_reduce_fusion, bf16[768,576]{0,1:T(8,128)(2,1)} %bitcast.86, bf16[576,1152]{1,0:T(8,128)(2,1)S(1)} %copy-done, f32[1152]{0:T(1024)S(1)} %get-tuple-element.3, bf16[1,768,1152]{2,1,0:T(8,128)(2,1)S(1)} %copy-done.1), kind=kOutput, calls=%fused_computation.19 | convolution fusion | flops 1023639552 | bytes 9298944 | tf_op jit(solution)/shard_map/dot_general | solution.py:112
  95.9 47.3 %all_to_all.8 = bf16[1,8,96,1152]{3,2,0,1:T(8,128)(2,1)S(1)} all-to-all(bf16[1,8,96,1152]{3,2,0,1:T(8,128)(2,1)S(1)} %bitcast.82), channel_id=1, replica_groups=mesh['groups'=2,'frame'=8,'band'=2] {'frame'}, dimensions={1} | all-to-all | bytes 3538944 | tf_op jit(solution)/shard_map/all_to_all | solution.py:119
  143.2 5.0 %convolution_convert_fusion = bf16[768,1728]{0,1:T(8,128)(2,1)} fusion(bf16[768,1152]{1,0:T(8,128)(2,1)S(1)} %bitcast.83, bf16[1152,1728]{0,1:T(8,128)(2,1)S(1)} %copy-done.9), kind=kOutput, calls=%fused_computation.20 | convolution fusion | flops 3058974720 | bytes 8404992 | tf_op jit(solution)/shard_map/dot_general | solution.py:122
  148.2 7.0 %reshape_reshape.3 = bf16[8,96,3,8,72]{1,0,4,3,2:T(8,128)(2,1)} reshape(bf16[768,1728]{0,1:T(8,128)(2,1)} %convolution_convert_fusion) | data formatting | bytes 5308416 | tf_op jit(solution)/shard_map/reshape;reshape | solution.py:36
  155.2 4.0 %fusion.44 = (bf16[8,96,1,8,72]{1,0,4,3,2:T(8,128)(2,1)}, bf16[8,96,1,8,72]{1,0,4,3,2:T(8,128)(2,1)}, bf16[8,96,1,8,72]{1,0,4,3,2:T(8,128)(2,1)}) fusion(bf16[8,96,3,8,72]{1,0,4,3,2:T(8,128)(2,1)} %reshape_reshape.3), kind=kLoop, calls=%fused_computation.78 | loop fusion | bytes 5308416 | tf_op jit(solution)/shard_map/slice | solution.py:44
  159.2 3.9 %copy.56 = bf16[8,96,1,8,72]{4,0,3,1,2:T(8,128)(2,1)S(1)} copy(bf16[8,96,1,8,72]{1,0,4,3,2:T(8,128)(2,1)} %get-tuple-element.11) | data formatting | bytes 1769472
  163.1 4.6 %copy.57 = bf16[8,96,1,8,72]{4,0,3,1,2:T(8,128)(2,1)} copy(bf16[8,96,1,8,72]{1,0,4,3,2:T(8,128)(2,1)} %get-tuple-element.12) | data formatting | bytes 1769472
  167.6 4.0 %fusion.19 = f32[96,8,8,8]{2,3,1,0:T(8,128)} fusion(bf16[8,96,1,8,72]{4,0,3,1,2:T(8,128)(2,1)} %copy.57, bf16[8,96,1,8,72]{4,0,3,1,2:T(8,128)(2,1)S(1)} %copy.56), kind=kOutput, calls=%fused_computation.33 | convolution fusion | flops 7077888 | bytes 1966080 | tf_op jit(solution)/shard_map/fnhd,gnhd->nhfg/dot_general | solution.py:37
  171.7 3.2 %copy.48 = f32[96,8,8,8]{0,3,2,1:T(8,128)S(1)} copy(f32[96,8,8,8]{2,3,1,0:T(8,128)} %fusion.19) | data formatting | bytes 393216 | tf_op jit(solution)/shard_map/fnhd,gnhd->nhfg/dot_general | solution.py:37
  175.0 2.9 %copy.49 = bf16[96,8,8,8]{3,2,1,0:T(8,128)(2,1)} copy(bf16[96,8,8,8]{0,3,2,1:T(8,128)(2,1)S(1)} %get-tuple-element.20) | data formatting | bytes 196608 | tf_op jit(solution)/shard_map/convert_element_type | solution.py:41
  178.2 3.4 %copy.55 = bf16[8,96,1,8,72]{4,0,3,1,2:T(8,128)(2,1)} copy(bf16[8,96,1,8,72]{1,0,4,3,2:T(8,128)(2,1)S(1)} %copy-done.3) | data formatting | bytes 1769472
  181.6 3.0 %fusion.10 = bf16[8,96,8,72]{3,0,2,1:T(8,128)(2,1)S(1)} fusion(bf16[96,8,8,8]{3,2,1,0:T(8,128)(2,1)} %copy.49, bf16[8,96,1,8,72]{4,0,3,1,2:T(8,128)(2,1)} %copy.55, f32[8,96,8]{0,2,1:T(8,128)S(1)} %copy.50), kind=kOutput, calls=%fused_computation.23 | convolution fusion | flops 7962624 | bytes 1892352 | tf_op jit(solution)/shard_map/nhfg,gnhd->fnhd/dot_general | solution.py:43
  184.8 2.5 %reshape_reshape_reshape.3 = bf16[8,1,48,1152]{3,2,0,1:T(8,128)(2,1)} reshape(bf16[8,96,8,72]{3,2,1,0:T(8,128)(2,1)S(1)} %copy.51) | data formatting | bytes 1769472 | tf_op jit(solution)/shard_map/reshape;reshape;reshape | solution.py:129
  187.3 3.8 %all-to-all-start.1 = ((bf16[8,1,48,1152]{3,2,1,0:T(8,128)(2,1)}), bf16[8,1,48,1152]{3,2,1,0:T(8,128)(2,1)S(1)}, u32[]{:S(2)}, u32[]{:S(2)}) async-start(bf16[8,1,48,1152]{3,2,1,0:T(8,128)(2,1)} %bitcast.80), calls=%async_computation.1 | async-start | bytes 1769472 | tf_op jit(solution)/shard_map/all_to_all | solution.py:130
  192.4 20.9 %all-to-all-done.1 = bf16[8,1,48,1152]{3,2,1,0:T(8,128)(2,1)S(1)} async-done(((bf16[8,1,48,1152]{3,2,1,0:T(8,128)(2,1)}), bf16[8,1,48,1152]{3,2,1,0:T(8,128)(2,1)S(1)}, u32[]{:S(2)}, u32[]{:S(2)}) %all-to-all-start.1) | async-done | bytes 884768 | tf_op jit(solution)/shard_map/all_to_all | solution.py:130
  213.9 4.1 %fusion.46 = (f32[768]{0:T(1024)S(1)}, f32[768,1152]{1,0:T(8,128)S(1)}) fusion(f32[768,1152]{1,0:T(8,128)} %get-tuple-element.18, bf16[768,576]{1,0:T(8,128)(2,1)S(1)} %reshape.171, bf16[576,1152]{1,0:T(8,128)(2,1)} %param.25, f32[1152]{0:T(1024)S(1)} %get-tuple-element.3), kind=kOutput, calls=%fused_computation.80 | convolution fusion | flops 1021869312 | bytes 9297408 | tf_op jit(solution)/shard_map/dot_general | solution.py:132
  218.1 1.8 multiply_reduce_fusion.1
  219.9 0.7 fusion.18
  220.8 3.1 %collective-permute-start = (bf16[1,96,128]{2,1,0:T(8,128)(2,1)S(1)}, bf16[1,96,128]{2,1,0:T(8,128)(2,1)S(1)}, u32[]{:S(2)}, u32[]{:S(2)}) collective-permute-start(bf16[1,96,128]{2,1,0:T(8,128)(2,1)S(1)} %add_convert_fusion.1), channel_id=1, source_target_pairs={{0,2},{2,4},{4,6},{6,8},{8,10},{10,12},{12,14},{1,3},{3,5},{5,7},{... | collective-permute-start | bytes 73736 | tf_op jit(solution)/shard_map/ppermute | solution.py:14
  224.0 1.5 collective-permute-done
  (41 shorter events, 3.0 us)
Async XLA Ops:
  7.2 83.8 %copy-start = (bf16[576,1152]{1,0:T(8,128)(2,1)S(1)}, bf16[576,1152]{1,0:T(8,128)(2,1)}, u32[]{:S(2)}) copy-start(bf16[576,1152]{1,0:T(8,128)(2,1)} %param.23) | copy-start | bytes 3981316
  7.2 7.1 %copy-start.1 = (bf16[1,768,1152]{2,1,0:T(8,128)(2,1)S(1)}, bf16[1,768,1152]{2,1,0:T(8,128)(2,1)}, u32[]{:S(2)}) copy-start(bf16[1,768,1152]{2,1,0:T(8,128)(2,1)} %param.14) | copy-start | bytes 5308420
  7.2 32.1 %all-gather.2.cloned.1.call-start = ((), (), s32[]{:S(2)}) async-start(), calls=%async_computation.2 | async-start | bytes 5308416 | tf_op jit(solution)/shard_map/all_gather | solution.py:92
  20.8 1.5 copy-start.2
  39.3 3.5 %slice-start = ((bf16[768,1728]{0,1:T(8,128)(2,1)}), bf16[768,576]{0,1:T(8,128)(2,1)S(1)}, s32[]{:S(2)}) async-start(bf16[768,1728]{0,1:T(8,128)(2,1)} %copy-done.2), calls=%async_computation.3 | async-start | bytes 1769472 | tf_op jit(solution)/shard_map/slice | solution.py:90
  91.0 52.3 %copy-start.9 = (bf16[1152,1728]{0,1:T(8,128)(2,1)S(1)}, bf16[1152,1728]{0,1:T(8,128)(2,1)}, u32[]{:S(2)}) copy-start(bf16[1152,1728]{0,1:T(8,128)(2,1)} %param.24) | copy-start | bytes 11943940
  171.6 6.5 %copy-start.3 = (bf16[8,96,1,8,72]{1,0,4,3,2:T(8,128)(2,1)S(1)}, bf16[8,96,1,8,72]{1,0,4,3,2:T(8,128)(2,1)}, u32[]{:S(2)}) copy-start(bf16[8,96,1,8,72]{1,0,4,3,2:T(8,128)(2,1)} %get-tuple-element.10) | copy-start | bytes 2654212
  187.3 26.0 %all-to-all-start.1 = ((bf16[8,1,48,1152]{3,2,1,0:T(8,128)(2,1)}), bf16[8,1,48,1152]{3,2,1,0:T(8,128)(2,1)S(1)}, u32[]{:S(2)}, u32[]{:S(2)}) async-start(bf16[8,1,48,1152]{3,2,1,0:T(8,128)(2,1)} %bitcast.80), calls=%async_computation.1 | async-start | bytes 1769472 | tf_op jit(solution)/shard_map/all_to_all | solution.py:130
  218.0 1.9 copy-start.7
  218.0 1.9 copy-start.8
  219.9 0.9 copy-start.5
  219.9 5.6 %copy-start.6 = (f32[96,128]{1,0:T(8,128)S(1)}, f32[96,128]{1,0:T(8,128)}, u32[]{:S(2)}) copy-start(f32[96,128]{1,0:T(8,128)} %param.16) | copy-start | bytes 147460
  220.8 5.3 %copy-start.4 = (f32[1,96,128]{2,1,0:T(8,128)}, f32[1,96,128]{2,1,0:T(8,128)S(1)}, u32[]{:S(2)}) copy-start(f32[1,96,128]{2,1,0:T(8,128)S(1)} %reshape.172) | copy-start | bytes 147460
  220.8 4.6 %collective-permute-start = (bf16[1,96,128]{2,1,0:T(8,128)(2,1)S(1)}, bf16[1,96,128]{2,1,0:T(8,128)(2,1)S(1)}, u32[]{:S(2)}, u32[]{:S(2)}) collective-permute-start(bf16[1,96,128]{2,1,0:T(8,128)(2,1)S(1)} %add_convert_fusion.1), channel_id=1, source_target_pairs={{0,2},{2,4},{4,6},{6,8},{8,10},{10,12},{12,14},{1,3},{3,5},{5,7},{... | collective-permute-start | bytes 73736 | tf_op jit(solution)/shard_map/ppermute | solution.py:14
Sparse Core Ops, SparseCore 0:
  23.8 15.4 all-gather.1
where the time goes:
time: 234 us; the launch traced here: 233 us
  matrix products  60.7 us (26%)
  blocking collectives  47.3 us (20%)
  local copies, waits for them, and re-layouts  38.9 us (17%)
  waiting for transfers between devices  37.1 us (16%)
  other arithmetic  24.2 us (10%)
  between operations  17.7 us (8%)
  starting transfers between devices  6.96 us (3%)
    all_to_all x1, blocking collectives, body(): lax.all_to_all(spread_rows, 'frame', split_axis=1, concat_axis=0, tiled=T...  47.3 us
    all_to_all x1, waiting for transfers between devices, body(): lax.all_to_all(mixed_pairs, 'frame', split_axis=0, concat_axis=1, tiled=T...  20.9 us
    reduce_sum x1, other arithmetic, body(): denominator = jnp.sum(attention_weight, axis=-1, dtype=jnp.float32)  16.7 us
    dot_general x1, matrix products, body(): jnp.einsum('leq,qlr->ler', attention_weight, value_matrix_rows, preferred...  16.7 us
    dot_general x1, matrix products, body(): jnp.einsum('ubg,wbg->buw', query_rows, key_matrix_rows, preferred_element...  14.8 us
    all_gather x1, waiting for transfers between devices, body(): block_rows = lax.all_gather(key_value, 'band', axis=0, tiled=True)  14.7 us
    unnamed x23, local copies, waits for them, and re-layouts  13.4 us
    another operation x1, local copies, waits for them, and re-layouts, mix_frames(): parted = rows.reshape(frame_count, item_count, 3, head_count, HEAD_SIZE)  6.97 us
  transfers between devices with their start and end apart: 3, of which 3 were waited for; matrix products, arithmetic and copies ran while one was open for 0% of the time, Pallas kernels for 0%

commit v1 on v0

--- a/solution.py
+++ b/solution.py
@@ -127,7 +127,12 @@
     mixed = mix_frames(rows.reshape(frame_count, item_count, 3 * attended), head_count)
     mixed_rows = mixed.reshape(frame_count, 1, item_count, attended)
     mixed_pairs = mixed_rows.reshape(mixed_rows.shape[0], 1, mixed_rows.shape[2] // 2, 2 * attended)
-    returned = lax.all_to_all(mixed_pairs, "frame", split_axis=0, concat_axis=1, tiled=True)
+    returned = jnp.concatenate(
+        lax.all_to_all(
+            jnp.stack(jnp.split(mixed_pairs, lax.axis_size("frame"), axis=0)), "frame", 0, 0
+        ),
+        axis=1,
+    )
     temporal_mixed = returned.reshape(tokens, attended)
     residual = residual + gate_part * jnp.dot(
         temporal_mixed, temporal_out, preferred_element_type=jnp.float32

time: 234 us -> 248 us (1.060)
  local copies, waits for them, and re-layouts: 38.9 us -> 52.7 us
    split x0 -> x1, local copies, waits for them, and re-layouts: none -> 9.47 us  [body(): jnp.split(mixed_pairs, lax.axis_size('frame'), axis=0)]
    unnamed x23 -> x30, local copies, waits for them, and re-layouts: 13.4 us -> 18 us
where the time goes in v1:
time: 248 us; the launch traced here: 247 us
  matrix products  60.7 us (24%)
  local copies, waits for them, and re-layouts  52.7 us (21%)
  blocking collectives  47.3 us (19%)
  waiting for transfers between devices  37.3 us (15%)
  other arithmetic  24.2 us (10%)
  between operations  17.7 us (7%)
  starting transfers between devices  6.84 us (3%)
    all_to_all x1, blocking collectives, body(): lax.all_to_all(spread_rows, 'frame', split_axis=1, concat_axis=0, tiled=T...  47.3 us
    all_to_all x1, waiting for transfers between devices, body(): lax.all_to_all(jnp.stack(jnp.split(mixed_pairs, lax.axis_size('frame'), a...  21 us
    unnamed x30, local copies, waits for them, and re-layouts  18 us
    reduce_sum x1, other arithmetic, body(): denominator = jnp.sum(attention_weight, axis=-1, dtype=jnp.float32)  16.7 us
    dot_general x1, matrix products, body(): jnp.einsum('leq,qlr->ler', attention_weight, value_matrix_rows, preferred...  16.7 us
    dot_general x1, matrix products, body(): jnp.einsum('ubg,wbg->buw', query_rows, key_matrix_rows, preferred_element...  14.8 us
    all_gather x1, waiting for transfers between devices, body(): block_rows = lax.all_gather(key_value, 'band', axis=0, tiled=True)  14.7 us
    split x1, local copies, waits for them, and re-layouts, body(): jnp.split(mixed_pairs, lax.axis_size('frame'), axis=0)  9.47 us
  transfers between devices with their start and end apart: 3, of which 3 were waited for; matrix products, arithmetic and copies ran while one was open for 0% of the time, Pallas kernels for 0%

profile of v1, /device:TPU:0, one launch (start us, length us, event | category | flops | bytes accessed | tf_op | source)
XLA Modules:
  0.0 246.7 jit_solution(10925627177147007724)
XLA Ops:
  8.0 1.4 fusion.32
  10.2 1.5 convolution_reduce_fusion
  11.7 0.7 add.73
  12.5 1.8 convert_reduce_fusion.1
  14.9 5.9 %convolution_convert_fusion.1 = bf16[768,1728]{0,1:T(8,128)(2,1)S(1)} fusion(bf16[1152,1728]{0,1:T(8,128)(2,1)} %param.22, bf16[1,768,1152]{2,1,0:T(8,128)(2,1)S(1)} %copy-done.1, f32[1152]{0:T(1024)S(1)} %get-tuple-element.12, f32[1152]{0:T(1024)S(1)} %get-tuple-element.13, f32[768]{0:T(1024)S(1)} %add_rsqrt_fusion.1, f32[768]{0:T(1024)S(1)} %broadcast_multiply_fusion.1), kind=kOutput, calls=%fused_computation.21 | convolution fusion | flops 3064283136 | bytes 8420352 | tf_op jit(solution)/shard_map/dot_general | solution.py:87
  20.8 1.5 copy-done.2
  22.3 1.3 slice.52
  24.5 14.7 %all-gather.2.cloned.1.call-done = bf16[1536,1152]{0,1:T(8,128)(2,1)} async-done(((bf16[768,1152]{0,1:T(8,128)(2,1)}), bf16[1536,1152]{0,1:T(8,128)(2,1)}) %all-gather.2.cloned.1.call-update) | async-done | bytes 3538960 | tf_op jit(solution)/shard_map/all_gather | solution.py:92
  39.3 3.5 %fusion.45 = (bf16[1536,576]{0,1:T(8,128)(2,1)S(1)}, bf16[1536,576]{0,1:T(8,128)(2,1)}) fusion(bf16[1536,1152]{0,1:T(8,128)(2,1)} %all-gather.2.cloned.1.call-done), kind=kLoop, calls=%fused_computation.95 | loop fusion | bytes 7077888 | tf_op jit(solution)/shard_map/slice | solution.py:95
  42.8 14.8 %multiply_reduce_fusion = (f32[8,768]{1,0:T(8,128)S(1)}, f32[8,768,1536]{2,1,0:T(8,128)}) fusion(bf16[768,8,72]{0,2,1:T(8,128)(2,1)S(1)} %bitcast.76, bf16[1536,8,72]{0,2,1:T(8,128)(2,1)S(1)} %bitcast.75), kind=kOutput, calls=%fused_computation.3 | convolution fusion | flops 1377822720 | bytes 40427520 | tf_op jit(solution)/shard_map/ubg,wbg->buw/dot_general | solution.py:97
  57.6 16.7 %convert_reduce_fusion = f32[8,768]{1,0:T(8,128)S(1)} fusion(f32[8,768]{1,0:T(8,128)S(1)} %broadcast_maximum_fusion, f32[8,768,1536]{2,1,0:T(8,128)} %get-tuple-element.24), kind=kLoop, calls=%fused_computation.1 | loop fusion | flops 47179776 | bytes 37797888 | tf_op jit(solution)/shard_map/reduce_sum | solution.py:102
  74.3 16.7 %fusion.13 = bf16[768,8,72]{0,2,1:T(8,128)(2,1)} fusion(bf16[1536,8,72]{0,2,1:T(8,128)(2,1)} %bitcast.77, f32[8,768,1536]{2,1,0:T(8,128)} %get-tuple-element.24, f32[8,768]{1,0:T(8,128)S(1)} %broadcast_maximum_fusion, f32[768,8]{0,1:T(8,128)S(1)} %bitcast.81), kind=kOutput, calls=%fused_computation.26 | convolution fusion | flops 1388150784 | bytes 40452096 | tf_op jit(solution)/shard_map/leq,qlr->ler/dot_general | solution.py:103
  91.0 5.0 %add_convert_fusion = (bf16[768,1152]{1,0:T(8,128)(2,1)S(1)}, f32[768,1152]{1,0:T(8,128)}) fusion(f32[1152]{0:T(1024)S(1)} %maximum_reduce_fusion, bf16[768,576]{0,1:T(8,128)(2,1)} %bitcast.82, bf16[576,1152]{1,0:T(8,128)(2,1)S(1)} %copy-done, f32[1152]{0:T(1024)S(1)} %get-tuple-element.11, bf16[1,768,1152]{2,1,0:T(8,128)(2,1)S(1)} %copy-done.1), kind=kOutput, calls=%fused_computation.19 | convolution fusion | flops 1023639552 | bytes 9298944 | tf_op jit(solution)/shard_map/dot_general | solution.py:112
  95.9 47.3 %all_to_all.14 = bf16[1,8,96,1152]{3,2,0,1:T(8,128)(2,1)S(1)} all-to-all(bf16[1,8,96,1152]{3,2,0,1:T(8,128)(2,1)S(1)} %bitcast.78), channel_id=1, replica_groups=mesh['groups'=2,'frame'=8,'band'=2] {'frame'}, dimensions={1} | all-to-all | bytes 3538944 | tf_op jit(solution)/shard_map/all_to_all | solution.py:119
  143.2 5.0 %convolution_convert_fusion = bf16[768,1728]{0,1:T(8,128)(2,1)} fusion(bf16[768,1152]{1,0:T(8,128)(2,1)S(1)} %bitcast.79, bf16[1152,1728]{0,1:T(8,128)(2,1)S(1)} %copy-done.9), kind=kOutput, calls=%fused_computation.20 | convolution fusion | flops 3058974720 | bytes 8404992 | tf_op jit(solution)/shard_map/dot_general | solution.py:122
  148.2 7.0 %reshape_reshape.6 = bf16[8,96,3,8,72]{1,0,4,3,2:T(8,128)(2,1)} reshape(bf16[768,1728]{0,1:T(8,128)(2,1)} %convolution_convert_fusion) | data formatting | bytes 5308416 | tf_op jit(solution)/shard_map/reshape;reshape | solution.py:36
  155.2 4.0 %fusion.44 = (bf16[8,96,1,8,72]{1,0,4,3,2:T(8,128)(2,1)}, bf16[8,96,1,8,72]{1,0,4,3,2:T(8,128)(2,1)}, bf16[8,96,1,8,72]{1,0,4,3,2:T(8,128)(2,1)}) fusion(bf16[8,96,3,8,72]{1,0,4,3,2:T(8,128)(2,1)} %reshape_reshape.6), kind=kLoop, calls=%fused_computation.94 | loop fusion | bytes 5308416 | tf_op jit(solution)/shard_map/slice | solution.py:44
  159.2 3.9 %copy.49 = bf16[8,96,1,8,72]{4,0,3,1,2:T(8,128)(2,1)S(1)} copy(bf16[8,96,1,8,72]{1,0,4,3,2:T(8,128)(2,1)} %get-tuple-element.19) | data formatting | bytes 1769472
  163.1 4.6 %copy.50 = bf16[8,96,1,8,72]{4,0,3,1,2:T(8,128)(2,1)} copy(bf16[8,96,1,8,72]{1,0,4,3,2:T(8,128)(2,1)} %get-tuple-element.20) | data formatting | bytes 1769472
  167.6 4.0 %fusion.19 = f32[96,8,8,8]{2,3,1,0:T(8,128)} fusion(bf16[8,96,1,8,72]{4,0,3,1,2:T(8,128)(2,1)} %copy.50, bf16[8,96,1,8,72]{4,0,3,1,2:T(8,128)(2,1)S(1)} %copy.49), kind=kOutput, calls=%fused_computation.33 | convolution fusion | flops 7077888 | bytes 1966080 | tf_op jit(solution)/shard_map/fnhd,gnhd->nhfg/dot_general | solution.py:37
  171.7 3.2 %copy.43 = f32[96,8,8,8]{0,3,2,1:T(8,128)S(1)} copy(f32[96,8,8,8]{2,3,1,0:T(8,128)} %fusion.19) | data formatting | bytes 393216 | tf_op jit(solution)/shard_map/fnhd,gnhd->nhfg/dot_general | solution.py:37
  175.0 2.9 %copy.44 = bf16[96,8,8,8]{3,2,1,0:T(8,128)(2,1)} copy(bf16[96,8,8,8]{0,3,2,1:T(8,128)(2,1)S(1)} %get-tuple-element.28) | data formatting | bytes 196608 | tf_op jit(solution)/shard_map/convert_element_type | solution.py:41
  178.2 3.4 %copy.48 = bf16[8,96,1,8,72]{4,0,3,1,2:T(8,128)(2,1)} copy(bf16[8,96,1,8,72]{1,0,4,3,2:T(8,128)(2,1)S(1)} %copy-done.3) | data formatting | bytes 1769472
  181.6 3.0 %fusion.10 = bf16[8,96,8,72]{3,0,2,1:T(8,128)(2,1)S(1)} fusion(bf16[96,8,8,8]{3,2,1,0:T(8,128)(2,1)} %copy.44, bf16[8,96,1,8,72]{4,0,3,1,2:T(8,128)(2,1)} %copy.48, f32[8,96,8]{0,2,1:T(8,128)S(1)} %copy.45), kind=kOutput, calls=%fused_computation.23 | convolution fusion | flops 7962624 | bytes 1892352 | tf_op jit(solution)/shard_map/nhfg,gnhd->fnhd/dot_general | solution.py:43
  184.6 9.5 %slice_reduce_fusion = (bf16[96,8,72]{2,1,0:T(8,128)(2,1)S(1)}, bf16[96,8,72]{2,1,0:T(8,128)(2,1)S(1)}, bf16[96,8,72]{2,1,0:T(8,128)(2,1)S(1)}, bf16[96,8,72]{2,...) fusion(bf16[8,96,8,72]{3,0,2,1:T(8,128)(2,1)S(1)} %fusion.10), kind=kLoop, calls=%fused_computation.41 | loop fusion | bytes 1769472 | tf_op jit(solution)/shard_map/split | solution.py:132
  201.1 3.6 %all-to-all-start.1 = ((bf16[8,1,1,48,1152]{4,3,2,1,0:T(8,128)(2,1)}), bf16[8,1,1,48,1152]{4,3,2,1,0:T(8,128)(2,1)S(1)}, u32[]{:S(2)}, u32[]{:S(2)}) async-start(bf16[8,1,1,48,1152]{4,3,2,1,0:T(8,128)(2,1)} %constant_dynamic-update-slice_fusion), calls=%async_computation.1 | async-start | bytes 1769472 | tf_op jit(solution)/shard_map/all_to_all | solution.py:131
  206.0 21.0 %all-to-all-done.1 = bf16[8,1,1,48,1152]{4,3,2,1,0:T(8,128)(2,1)S(1)} async-done(((bf16[8,1,1,48,1152]{4,3,2,1,0:T(8,128)(2,1)}), bf16[8,1,1,48,1152]{4,3,2,1,0:T(8,128)(2,1)S(1)}, u32[]{:S(2)}, u32[]{:S(2)}) %all-to-all-start.1) | async-done | bytes 884768 | tf_op jit(solution)/shard_map/all_to_all | solution.py:131
  227.6 4.1 %fusion.46 = (f32[768]{0:T(1024)S(1)}, f32[768,1152]{1,0:T(8,128)S(1)}) fusion(f32[768,1152]{1,0:T(8,128)} %get-tuple-element.26, bf16[768,576]{1,0:T(8,128)(2,1)S(1)} %reshape_reshape.7, bf16[576,1152]{1,0:T(8,128)(2,1)} %param.25, f32[1152]{0:T(1024)S(1)} %get-tuple-element.11), kind=kOutput, calls=%fused_computation.96 | convolution fusion | flops 1021869312 | bytes 9297408 | tf_op jit(solution)/shard_map/dot_general | solution.py:137
  231.7 1.8 multiply_reduce_fusion.1
  233.6 0.7 fusion.18
  234.5 3.2 %collective-permute-start = (bf16[1,96,128]{2,1,0:T(8,128)(2,1)S(1)}, bf16[1,96,128]{2,1,0:T(8,128)(2,1)S(1)}, u32[]{:S(2)}, u32[]{:S(2)}) collective-permute-start(bf16[1,96,128]{2,1,0:T(8,128)(2,1)S(1)} %add_convert_fusion.1), channel_id=1, source_target_pairs={{0,2},{2,4},{4,6},{6,8},{8,10},{10,12},{12,14},{1,3},{3,5},{5,7},{... | collective-permute-start | bytes 73736 | tf_op jit(solution)/shard_map/ppermute | solution.py:14
  237.8 1.5 collective-permute-done
  (56 shorter events, 9.8 us)
Async XLA Ops:
  7.2 83.8 %copy-start = (bf16[576,1152]{1,0:T(8,128)(2,1)S(1)}, bf16[576,1152]{1,0:T(8,128)(2,1)}, u32[]{:S(2)}) copy-start(bf16[576,1152]{1,0:T(8,128)(2,1)} %param.23) | copy-start | bytes 3981316
  7.2 7.1 %copy-start.1 = (bf16[1,768,1152]{2,1,0:T(8,128)(2,1)S(1)}, bf16[1,768,1152]{2,1,0:T(8,128)(2,1)}, u32[]{:S(2)}) copy-start(bf16[1,768,1152]{2,1,0:T(8,128)(2,1)} %param.14) | copy-start | bytes 5308420
  7.2 32.1 %all-gather.2.cloned.1.call-start = ((), (), s32[]{:S(2)}) async-start(), calls=%async_computation.2 | async-start | bytes 5308416 | tf_op jit(solution)/shard_map/all_gather | solution.py:92
  20.8 1.5 copy-start.2
  39.3 3.5 %slice-start = ((bf16[768,1728]{0,1:T(8,128)(2,1)}), bf16[768,576]{0,1:T(8,128)(2,1)S(1)}, s32[]{:S(2)}) async-start(bf16[768,1728]{0,1:T(8,128)(2,1)} %copy-done.2), calls=%async_computation.3 | async-start | bytes 1769472 | tf_op jit(solution)/shard_map/slice | solution.py:90
  91.0 52.3 %copy-start.9 = (bf16[1152,1728]{0,1:T(8,128)(2,1)S(1)}, bf16[1152,1728]{0,1:T(8,128)(2,1)}, u32[]{:S(2)}) copy-start(bf16[1152,1728]{0,1:T(8,128)(2,1)} %param.24) | copy-start | bytes 11943940
  171.6 6.5 %copy-start.3 = (bf16[8,96,1,8,72]{1,0,4,3,2:T(8,128)(2,1)S(1)}, bf16[8,96,1,8,72]{1,0,4,3,2:T(8,128)(2,1)}, u32[]{:S(2)}) copy-start(bf16[8,96,1,8,72]{1,0,4,3,2:T(8,128)(2,1)} %get-tuple-element.18) | copy-start | bytes 2654212
  201.1 25.9 %all-to-all-start.1 = ((bf16[8,1,1,48,1152]{4,3,2,1,0:T(8,128)(2,1)}), bf16[8,1,1,48,1152]{4,3,2,1,0:T(8,128)(2,1)S(1)}, u32[]{:S(2)}, u32[]{:S(2)}) async-start(bf16[8,1,1,48,1152]{4,3,2,1,0:T(8,128)(2,1)} %constant_dynamic-update-slice_fusion), calls=%async_computation.1 | async-start | bytes 1769472 | tf_op jit(solution)/shard_map/all_to_all | solution.py:131
  231.7 1.9 copy-start.7
  231.7 1.9 copy-start.8
  233.5 0.9 copy-start.5
  233.5 5.7 %copy-start.6 = (f32[96,128]{1,0:T(8,128)S(1)}, f32[96,128]{1,0:T(8,128)}, u32[]{:S(2)}) copy-start(f32[96,128]{1,0:T(8,128)} %param.16) | copy-start | bytes 147460
  234.5 5.4 %copy-start.4 = (f32[1,96,128]{2,1,0:T(8,128)}, f32[1,96,128]{2,1,0:T(8,128)S(1)}, u32[]{:S(2)}) copy-start(f32[1,96,128]{2,1,0:T(8,128)S(1)} %reshape.180) | copy-start | bytes 147460
  234.5 4.8 %collective-permute-start = (bf16[1,96,128]{2,1,0:T(8,128)(2,1)S(1)}, bf16[1,96,128]{2,1,0:T(8,128)(2,1)S(1)}, u32[]{:S(2)}, u32[]{:S(2)}) collective-permute-start(bf16[1,96,128]{2,1,0:T(8,128)(2,1)S(1)} %add_convert_fusion.1), channel_id=1, source_target_pairs={{0,2},{2,4},{4,6},{6,8},{8,10},{10,12},{12,14},{1,3},{3,5},{5,7},{... | collective-permute-start | bytes 73736 | tf_op jit(solution)/shard_map/ppermute | solution.py:14
Sparse Core Ops, SparseCore 0:
  23.8 15.4 all-gather.1
